TPU v7x, 256 devices: a whole 4x4x8 slice. The times are simulated.
256 devices in a mesh: rows: 32 (over y, x, core), hub: 8 (over z).
Axes of the slice: x: 4, y: 4, z: 8, core: 2. Of those that a mesh axis runs over, the one named last changes fastest.
Arguments:
- tail_blocks: float32 [18432, 128, 128], P(('rows', 'hub')), may hold values from -0.21875 to 0.21875
- tail_row: int32 [18432], P(('rows', 'hub')), may hold values from 0 to 15
- tail_owner: int32 [18432, 1], P(('rows', 'hub')), may hold values from 0 to 31; in each aligned block of 72 rows (0 to 71, 72 to 143, ...) at most 6 rows name the same one
- tail_slot: int32 [18432], P(('rows', 'hub')), may hold values from 0 to 63
- hub_blocks: float32 [6144, 128, 128], P(('rows', 'hub')), may hold values from -0.21875 to 0.21875
- hub_row: int32 [6144], P(('rows', 'hub')), may hold values from 0 to 15
- hub_col: int32 [6144], P(('rows', 'hub')), may hold values from 0 to 255
- x_tail: float32 [16384, 128], P(('rows', 'hub')), may hold values from 0 to 0.5
- cost_tail: float32 [16384, 128], P(('rows', 'hub')), may hold values from -6 to 6
- upper_tail: float32 [16384, 128], P(('rows', 'hub')), may hold values from 0.5 to 2
- x_hub: float32 [256, 128], P('hub'), may hold values from 0 to 0.5
- cost_hub: float32 [256, 128], P('hub'), may hold values from -6 to 6
- upper_hub: float32 [256, 128], P('hub'), may hold values from 0.5 to 2
- duals: float32 [4096, 128], P(('rows', 'hub')), may hold values from 0 to 1
- demand: float32 [4096, 128], P(('rows', 'hub')), may hold values from -6 to 6
Outputs:
- x_tail_out: float32 [16384, 128], P(('rows', 'hub'))
- x_hub_out: float32 [256, 128], P('hub')
- duals_out: float32 [4096, 128], P(('rows', 'hub'))
Inputs may be any that keep to these rules, and one draw needn't show every extreme that they name: `tail_owner`: among the blocks of one device no owner is named more than 6 times; on some device one owner is named exactly 6 times.
All inputs are finite; a program needn't handle non-finite values.
Results may differ from a plain program's by a relative error of at most 0.0001.
Values sent between devices are 32-bit elements; how exact they have to be, the bound alone decides.
A program may use at most 64 MiB of HBM per device.

v0:
```python
import jax
import jax.numpy as jnp
from jax import lax
from jax.sharding import PartitionSpec as P

ITERS = 3


primal_step = 0.25
dual_step = 0.25


def split_up(shard, dim, peers):
    before, after = (shard.shape[:dim], shard.shape[dim + 1 :])
    return jnp.moveaxis(shard.reshape(*before, peers, -1, *after), dim, 0)


def sum_at_owner(shard, axis, dim):
    pieces = split_up(shard, dim, lax.axis_size(axis))
    arrived = lax.all_to_all(pieces, axis, split_axis=0, concat_axis=0, tiled=True)
    return arrived.sum(axis=0)


def from_everyone(shard, axis):
    copies = jnp.broadcast_to(shard, (lax.axis_size(axis), *shard.shape))
    return lax.all_to_all(copies, axis, split_axis=0, concat_axis=0, tiled=True)


def of_everyone(shard, axis):
    return from_everyone(shard, axis).sum(axis=0)


def in_order(pieces, dim):
    lengths = list(pieces.shape[1:])
    lengths[dim] *= pieces.shape[0]
    return jnp.moveaxis(pieces, 0, dim).reshape(lengths)


def gather_directly(shard, axis, dim):
    pieces = from_everyone(shard, axis)
    return in_order(pieces, dim)


def on_device(
    tail_blocks,
    tail_row,
    tail_owner,
    tail_slot,
    hub_blocks,
    hub_row,
    hub_col,
    x_tail,
    cost_tail,
    upper_tail,
    x_hub,
    cost_hub,
    upper_hub,
    duals,
    demand,
):
    highest = lax.Precision.HIGHEST
    row_devs = lax.axis_size("rows")
    hub_devs = lax.axis_size("hub")
    tail_count = tail_blocks.shape[0]
    col_blocks = x_tail.shape[0]
    row_blocks = duals.shape[0]
    hub_share = x_hub.shape[0]
    hub_total = hub_share * hub_devs
    width = x_tail.shape[1]
    capacity = max(2, 3 * tail_count // row_devs)
    owners = tail_owner[:, 0]
    hits = (owners[:, None] == jnp.arange(row_devs, dtype=jnp.int32)[None, :]).astype(jnp.int32)
    within = jnp.sum(jnp.cumsum(hits, axis=0) * hits, axis=1) - 1
    places = owners * capacity + within
    asked_slots = jnp.zeros((row_devs * capacity,), jnp.int32).at[places].set(tail_slot)
    requested = lax.all_to_all(
        asked_slots.reshape(row_devs, capacity), "rows", split_axis=0, concat_axis=0, tiled=True
    ).reshape(-1)
    collector = (jnp.arange(col_blocks, dtype=jnp.int32)[:, None] == requested[None, :]).astype(
        jnp.float32
    )
    tail_rowpick = (jnp.arange(row_blocks, dtype=jnp.int32)[:, None] == tail_row[None, :]).astype(
        jnp.float32
    )
    hub_rowpick = (jnp.arange(row_blocks, dtype=jnp.int32)[:, None] == hub_row[None, :]).astype(
        jnp.float32
    )
    hub_state = x_hub
    hub_pick = (jnp.arange(hub_total, dtype=jnp.int32)[:, None] == hub_col[None, :]).astype(
        jnp.float32
    )
    tail_state = x_tail
    for iteration in range(ITERS):
        tail_terms = jnp.einsum("bij,bi->bj", tail_blocks, duals[tail_row], precision=highest)
        outgoing = jnp.zeros((row_devs * capacity, width), jnp.float32).at[places].set(tail_terms)
        arrived = lax.all_to_all(
            outgoing.reshape(row_devs, capacity, width),
            "rows",
            split_axis=0,
            concat_axis=0,
            tiled=True,
        )
        tail_image = jnp.dot(
            collector,
            arrived.reshape(-1, width),
            precision=highest,
            preferred_element_type=jnp.float32,
        )
        tail_next = jnp.minimum(
            jnp.maximum(tail_state - primal_step * (cost_tail - tail_image), 0.0), upper_tail
        )
        tail_extra = 2.0 * tail_next - tail_state
        hub_terms = jnp.einsum("bij,bi->bj", hub_blocks, duals[hub_row], precision=highest)
        hub_partial = jnp.dot(
            hub_pick, hub_terms, precision=highest, preferred_element_type=jnp.float32
        )
        hub_sums = sum_at_owner(hub_partial, "hub", 0)
        hub_sums = of_everyone(hub_sums, "rows")
        hub_next = jnp.minimum(
            jnp.maximum(hub_state - primal_step * (cost_hub - hub_sums), 0.0), upper_hub
        )
        hub_extra = 2.0 * hub_next - hub_state
        hub_full = gather_directly(hub_extra, "hub", 0)
        answers = tail_extra[requested].reshape(row_devs, capacity, width)
        returned = lax.all_to_all(answers, "rows", split_axis=0, concat_axis=0, tiled=True)
        tail_picked = returned.reshape(-1, width)[places]
        tail_product = jnp.einsum("bij,bj->bi", tail_blocks, tail_picked, precision=highest)
        hub_product = jnp.einsum("bij,bj->bi", hub_blocks, hub_full[hub_col], precision=highest)
        primal_image = jnp.dot(
            tail_rowpick, tail_product, precision=highest, preferred_element_type=jnp.float32
        )
        primal_image = primal_image + jnp.dot(
            hub_rowpick, hub_product, precision=highest, preferred_element_type=jnp.float32
        )
        duals = jnp.maximum(duals + dual_step * (demand - primal_image), 0.0)
        tail_state = tail_next
        hub_state = hub_next
    return (tail_state, hub_state, duals)


def solution(mesh):
    in_specs = (
        P(("rows", "hub"), None, None),
        P(("rows", "hub")),
        P(("rows", "hub"), None),
        P(("rows", "hub")),
        P(("rows", "hub"), None, None),
        P(("rows", "hub")),
        P(("rows", "hub")),
        P(("rows", "hub"), None),
        P(("rows", "hub"), None),
        P(("rows", "hub"), None),
        P("hub", None),
        P("hub", None),
        P("hub", None),
        P(("rows", "hub"), None),
        P(("rows", "hub"), None),
    )
    out_specs = (P(("rows", "hub"), None), P("hub", None), P(("rows", "hub"), None))
    return jax.shard_map(
        on_device, mesh=mesh, in_specs=in_specs, out_specs=out_specs, check_vma=False
    )
```

profile of v0, /device:TPU:1, one launch (start us, length us, event | category | flops | bytes accessed | tf_op | source)
XLA Modules:
  0.0 271.2 jit_solution(11737158733228618677)
XLA Ops:
  4.8 8.6 %all-to-all-start = ((s32[32,1,6]{2,1,0:T(1,128)}), s32[32,1,6]{2,1,0:T(1,128)S(1)}, u32[]{:S(2)}, u32[]{:S(2)}) async-start(s32[32,1,6]{2,1,0:T(1,128)} %bitcast.3), calls=%async_computation | async-start | bytes 32768 | tf_op jit(solution)/shard_map/all_to_all | solution.py:76
  18.7 5.8 %fusion.52 = f32[72,1,128]{2,1,0:T(1,128)S(1)} fusion(f32[72,128,1]{1,2,0:T(1,128)S(1)} %bitcast.126, f32[72,128,128]{2,1,0:T(8,128)} %param.15), kind=kOutput, calls=%fused_computation.103 | convolution fusion | flops 14155776 | bytes 4792320 | tf_op jit(solution)/shard_map/bij,bi->bj/dot_general | solution.py:94
  26.9 7.4 %all-to-all-start.1 = ((f32[32,6,128]{2,1,0:T(8,128)}), f32[32,6,128]{2,1,0:T(8,128)S(1)}, u32[]{:S(2)}, u32[]{:S(2)}) async-start(f32[32,6,128]{2,1,0:T(8,128)} %reshape.110), calls=%async_computation.1 | async-start | bytes 262144 | tf_op jit(solution)/shard_map/all_to_all | solution.py:96
  35.7 6.2 %all-to-all-done.1 = f32[32,6,128]{2,1,0:T(8,128)S(1)} async-done(((f32[32,6,128]{2,1,0:T(8,128)}), f32[32,6,128]{2,1,0:T(8,128)S(1)}, u32[]{:S(2)}, u32[]{:S(2)}) %all-to-all-start.1) | async-done | bytes 98336 | tf_op jit(solution)/shard_map/all_to_all | solution.py:96
  41.8 8.2 %all-to-all-start.3 = ((f32[8,32,128]{2,1,0:T(8,128)}), f32[8,32,128]{2,1,0:T(8,128)S(1)}, u32[]{:S(2)}, u32[]{:S(2)}) async-start(f32[8,32,128]{2,1,0:T(8,128)} %bitcast.17), calls=%async_computation.3 | async-start | bytes 262144 | tf_op jit(solution)/shard_map/all_to_all | solution.py:20
  51.6 6.2 %all-to-all-done.3 = f32[8,32,128]{2,1,0:T(8,128)S(1)} async-done(((f32[8,32,128]{2,1,0:T(8,128)}), f32[8,32,128]{2,1,0:T(8,128)S(1)}, u32[]{:S(2)}, u32[]{:S(2)}) %all-to-all-start.3) | async-done | bytes 131104 | tf_op jit(solution)/shard_map/all_to_all | solution.py:20
  57.9 5.7 %all-to-all-start.2 = ((f32[32,6,128]{2,1,0:T(8,128)}), f32[32,6,128]{2,1,0:T(8,128)S(1)}, u32[]{:S(2)}, u32[]{:S(2)}) async-start(f32[32,6,128]{2,1,0:T(8,128)} %reshape.113), calls=%async_computation.2 | async-start | bytes 262144 | tf_op jit(solution)/shard_map/all_to_all | solution.py:125
  63.6 7.7 %all-to-all-done.2 = f32[32,6,128]{2,1,0:T(8,128)S(1)} async-done(((f32[32,6,128]{2,1,0:T(8,128)}), f32[32,6,128]{2,1,0:T(8,128)S(1)}, u32[]{:S(2)}, u32[]{:S(2)}) %all-to-all-start.2) | async-done | bytes 98336 | tf_op jit(solution)/shard_map/all_to_all | solution.py:125
  76.9 10.9 %all-to-all-done.4 = f32[32,32,128]{2,1,0:T(8,128)S(1)} async-done(((f32[32,32,128]{2,1,0:T(8,128)}), f32[32,32,128]{2,1,0:T(8,128)S(1)}, u32[]{:S(2)}, u32[]{:S(2)}) %all-to-all-start.4) | async-done | bytes 524320 | tf_op jit(solution)/shard_map/all_to_all | solution.py:26
  92.1 9.2 %fusion.53 = f32[72,1,128]{2,1,0:T(1,128)S(1)} fusion(f32[72,128,1]{1,2,0:T(1,128)S(1)} %bitcast.124, f32[72,128,128]{2,1,0:T(8,128)} %param.15), kind=kOutput, calls=%fused_computation.104 | convolution fusion | flops 14155776 | bytes 4792320 | tf_op jit(solution)/shard_map/bij,bj->bi/dot_general | solution.py:127
  107.3 5.8 %fusion.56 = f32[72,1,128]{2,1,0:T(1,128)S(1)} fusion(f32[72,128,1]{1,2,0:T(1,128)S(1)} %bitcast.127, f32[72,128,128]{2,1,0:T(8,128)} %param.15), kind=kOutput, calls=%fused_computation.107 | convolution fusion | flops 14155776 | bytes 4792320 | tf_op jit(solution)/shard_map/bij,bi->bj/dot_general | solution.py:94
  119.4 6.8 %all-to-all-done.6 = f32[32,6,128]{2,1,0:T(8,128)S(1)} async-done(((f32[32,6,128]{2,1,0:T(8,128)}), f32[32,6,128]{2,1,0:T(8,128)S(1)}, u32[]{:S(2)}, u32[]{:S(2)}) %all-to-all-start.6) | async-done | bytes 98336 | tf_op jit(solution)/shard_map/all_to_all | solution.py:96
  126.2 6.7 %all-to-all-start.8 = ((f32[8,32,128]{2,1,0:T(8,128)}), f32[8,32,128]{2,1,0:T(8,128)S(1)}, u32[]{:S(2)}, u32[]{:S(2)}) async-start(f32[8,32,128]{2,1,0:T(8,128)} %bitcast.35), calls=%async_computation.8 | async-start | bytes 262144 | tf_op jit(solution)/shard_map/all_to_all | solution.py:20
  134.4 6.3 %all-to-all-done.8 = f32[8,32,128]{2,1,0:T(8,128)S(1)} async-done(((f32[8,32,128]{2,1,0:T(8,128)}), f32[8,32,128]{2,1,0:T(8,128)S(1)}, u32[]{:S(2)}, u32[]{:S(2)}) %all-to-all-start.8) | async-done | bytes 131104 | tf_op jit(solution)/shard_map/all_to_all | solution.py:20
  146.4 7.7 %all-to-all-done.7 = f32[32,6,128]{2,1,0:T(8,128)S(1)} async-done(((f32[32,6,128]{2,1,0:T(8,128)}), f32[32,6,128]{2,1,0:T(8,128)S(1)}, u32[]{:S(2)}, u32[]{:S(2)}) %all-to-all-start.7) | async-done | bytes 98336 | tf_op jit(solution)/shard_map/all_to_all | solution.py:125
  159.5 10.9 %all-to-all-done.9 = f32[32,32,128]{2,1,0:T(8,128)S(1)} async-done(((f32[32,32,128]{2,1,0:T(8,128)}), f32[32,32,128]{2,1,0:T(8,128)S(1)}, u32[]{:S(2)}, u32[]{:S(2)}) %all-to-all-start.9) | async-done | bytes 524320 | tf_op jit(solution)/shard_map/all_to_all | solution.py:26
  174.7 9.2 %fusion.57 = f32[72,1,128]{2,1,0:T(1,128)S(1)} fusion(f32[72,128,1]{1,2,0:T(1,128)S(1)} %bitcast.123, f32[72,128,128]{2,1,0:T(8,128)} %param.15), kind=kOutput, calls=%fused_computation.108 | convolution fusion | flops 14155776 | bytes 4792320 | tf_op jit(solution)/shard_map/bij,bj->bi/dot_general | solution.py:127
  189.9 5.8 %fusion.60 = f32[72,1,128]{2,1,0:T(1,128)S(1)} fusion(f32[72,128,1]{1,2,0:T(1,128)S(1)} %bitcast.125, f32[72,128,128]{2,1,0:T(8,128)} %param.15), kind=kOutput, calls=%fused_computation.111 | convolution fusion | flops 14155776 | bytes 4792320 | tf_op jit(solution)/shard_map/bij,bi->bj/dot_general | solution.py:94
  202.0 6.8 %all-to-all-done.11 = f32[32,6,128]{2,1,0:T(8,128)S(1)} async-done(((f32[32,6,128]{2,1,0:T(8,128)}), f32[32,6,128]{2,1,0:T(8,128)S(1)}, u32[]{:S(2)}, u32[]{:S(2)}) %all-to-all-start.11) | async-done | bytes 98336 | tf_op jit(solution)/shard_map/all_to_all | solution.py:96
  208.8 6.6 %all-to-all-start.12 = ((f32[8,32,128]{2,1,0:T(8,128)}), f32[8,32,128]{2,1,0:T(8,128)S(1)}, u32[]{:S(2)}, u32[]{:S(2)}) async-start(f32[8,32,128]{2,1,0:T(8,128)} %bitcast.49), calls=%async_computation.12 | async-start | bytes 262144 | tf_op jit(solution)/shard_map/all_to_all | solution.py:20
  223.3 5.7 %all-to-all-start.14 = ((f32[32,6,128]{2,1,0:T(8,128)}), f32[32,6,128]{2,1,0:T(8,128)S(1)}, u32[]{:S(2)}, u32[]{:S(2)}) async-start(f32[32,6,128]{2,1,0:T(8,128)} %reshape.126), calls=%async_computation.14 | async-start | bytes 262144 | tf_op jit(solution)/shard_map/all_to_all | solution.py:125
  229.0 7.7 %all-to-all-done.14 = f32[32,6,128]{2,1,0:T(8,128)S(1)} async-done(((f32[32,6,128]{2,1,0:T(8,128)}), f32[32,6,128]{2,1,0:T(8,128)S(1)}, u32[]{:S(2)}, u32[]{:S(2)}) %all-to-all-start.14) | async-done | bytes 98336 | tf_op jit(solution)/shard_map/all_to_all | solution.py:125
  242.1 10.9 %all-to-all-done.13 = f32[32,32,128]{2,1,0:T(8,128)S(1)} async-done(((f32[32,32,128]{2,1,0:T(8,128)}), f32[32,32,128]{2,1,0:T(8,128)S(1)}, u32[]{:S(2)}, u32[]{:S(2)}) %all-to-all-start.13) | async-done | bytes 524320 | tf_op jit(solution)/shard_map/all_to_all | solution.py:26
  258.0 9.2 %fusion.62 = f32[72,1,128]{2,1,0:T(1,128)S(1)} fusion(f32[72,128,1]{1,2,0:T(1,128)S(1)} %bitcast.122, f32[72,128,128]{2,1,0:T(8,128)} %param.15), kind=kOutput, calls=%fused_computation.113 | convolution fusion | flops 14155776 | bytes 4792320 | tf_op jit(solution)/shard_map/bij,bj->bi/dot_general | solution.py:127
  (120 shorter events, 88.4 us)
Async XLA Ops:
  0.7 49.4 %copy-start.2 = (f32[64,128]{1,0:T(8,128)S(1)}, f32[64,128]{1,0:T(8,128)}, u32[]{:S(2)}) copy-start(f32[64,128]{1,0:T(8,128)} %param.24) | copy-start | bytes 98308
  0.7 49.4 %copy-start.3 = (f32[64,128]{1,0:T(8,128)S(1)}, f32[64,128]{1,0:T(8,128)}, u32[]{:S(2)}) copy-start(f32[64,128]{1,0:T(8,128)} %param.23) | copy-start | bytes 98308
  0.7 49.4 %copy-start.7 = (f32[64,128]{1,0:T(8,128)S(1)}, f32[64,128]{1,0:T(8,128)}, u32[]{:S(2)}) copy-start(f32[64,128]{1,0:T(8,128)} %param.22) | copy-start | bytes 98308
  4.8 22.1 %all-to-all-start = ((s32[32,1,6]{2,1,0:T(1,128)}), s32[32,1,6]{2,1,0:T(1,128)S(1)}, u32[]{:S(2)}, u32[]{:S(2)}) async-start(s32[32,1,6]{2,1,0:T(1,128)} %bitcast.3), calls=%async_computation | async-start | bytes 32768 | tf_op jit(solution)/shard_map/all_to_all | solution.py:76
  18.7 69.1 %copy-start.4 = (f32[32,128]{1,0:T(8,128)S(1)}, f32[32,128]{1,0:T(8,128)}, u32[]{:S(2)}) copy-start(f32[32,128]{1,0:T(8,128)} %param.27) | copy-start | bytes 49156
  18.7 69.1 %copy-start.5 = (f32[32,128]{1,0:T(8,128)S(1)}, f32[32,128]{1,0:T(8,128)}, u32[]{:S(2)}) copy-start(f32[32,128]{1,0:T(8,128)} %param.26) | copy-start | bytes 49156
  18.7 69.1 %copy-start.8 = (f32[32,128]{1,0:T(8,128)S(1)}, f32[32,128]{1,0:T(8,128)}, u32[]{:S(2)}) copy-start(f32[32,128]{1,0:T(8,128)} %param.25) | copy-start | bytes 49156
  26.9 15.0 %all-to-all-start.1 = ((f32[32,6,128]{2,1,0:T(8,128)}), f32[32,6,128]{2,1,0:T(8,128)S(1)}, u32[]{:S(2)}, u32[]{:S(2)}) async-start(f32[32,6,128]{2,1,0:T(8,128)} %reshape.110), calls=%async_computation.1 | async-start | bytes 262144 | tf_op jit(solution)/shard_map/all_to_all | solution.py:96
  41.8 16.0 %all-to-all-start.3 = ((f32[8,32,128]{2,1,0:T(8,128)}), f32[8,32,128]{2,1,0:T(8,128)S(1)}, u32[]{:S(2)}, u32[]{:S(2)}) async-start(f32[8,32,128]{2,1,0:T(8,128)} %bitcast.17), calls=%async_computation.3 | async-start | bytes 262144 | tf_op jit(solution)/shard_map/all_to_all | solution.py:20
  50.3 51.0 %copy-start.10 = (s32[72]{0:T(128)S(1)}, s32[72]{0:T(128)}, u32[]{:S(2)}) copy-start(s32[72]{0:T(128)} %param.16) | copy-start | bytes 868
  57.9 13.4 %all-to-all-start.2 = ((f32[32,6,128]{2,1,0:T(8,128)}), f32[32,6,128]{2,1,0:T(8,128)S(1)}, u32[]{:S(2)}, u32[]{:S(2)}) async-start(f32[32,6,128]{2,1,0:T(8,128)} %reshape.113), calls=%async_computation.2 | async-start | bytes 262144 | tf_op jit(solution)/shard_map/all_to_all | solution.py:125
  72.1 32.4 %copy-start.11 = (s32[24]{0:T(128)S(1)}, s32[24]{0:T(128)}, u32[]{:S(2)}) copy-start(s32[24]{0:T(128)} %param.20) | copy-start | bytes 292
  72.1 15.6 %all-to-all-start.4 = ((f32[32,32,128]{2,1,0:T(8,128)}), f32[32,32,128]{2,1,0:T(8,128)S(1)}, u32[]{:S(2)}, u32[]{:S(2)}) async-start(f32[32,32,128]{2,1,0:T(8,128)} %broadcast_in_dim.20), calls=%async_computation.4 | async-start | bytes 1048576 | tf_op jit(solution)/shard_map/all_to_all | solution.py:26
  88.5 12.9 %all-to-all-start.5 = ((f32[8,32,128]{2,1,0:T(8,128)}), f32[8,32,128]{2,1,0:T(8,128)S(1)}, u32[]{:S(2)}, u32[]{:S(2)}) async-start(f32[8,32,128]{2,1,0:T(8,128)} %broadcast_in_dim.21), calls=%async_computation.5 | async-start | bytes 262144 | tf_op jit(solution)/shard_map/all_to_all | solution.py:26
  114.6 11.6 %all-to-all-start.6 = ((f32[32,6,128]{2,1,0:T(8,128)}), f32[32,6,128]{2,1,0:T(8,128)S(1)}, u32[]{:S(2)}, u32[]{:S(2)}) async-start(f32[32,6,128]{2,1,0:T(8,128)} %reshape.117), calls=%async_computation.6 | async-start | bytes 262144 | tf_op jit(solution)/shard_map/all_to_all | solution.py:96
  126.2 14.5 %all-to-all-start.8 = ((f32[8,32,128]{2,1,0:T(8,128)}), f32[8,32,128]{2,1,0:T(8,128)S(1)}, u32[]{:S(2)}, u32[]{:S(2)}) async-start(f32[8,32,128]{2,1,0:T(8,128)} %bitcast.35), calls=%async_computation.8 | async-start | bytes 262144 | tf_op jit(solution)/shard_map/all_to_all | solution.py:20
  140.7 13.4 %all-to-all-start.7 = ((f32[32,6,128]{2,1,0:T(8,128)}), f32[32,6,128]{2,1,0:T(8,128)S(1)}, u32[]{:S(2)}, u32[]{:S(2)}) async-start(f32[32,6,128]{2,1,0:T(8,128)} %reshape.119), calls=%async_computation.7 | async-start | bytes 262144 | tf_op jit(solution)/shard_map/all_to_all | solution.py:125
  154.9 15.5 %all-to-all-start.9 = ((f32[32,32,128]{2,1,0:T(8,128)}), f32[32,32,128]{2,1,0:T(8,128)S(1)}, u32[]{:S(2)}, u32[]{:S(2)}) async-start(f32[32,32,128]{2,1,0:T(8,128)} %broadcast_in_dim.23), calls=%async_computation.9 | async-start | bytes 1048576 | tf_op jit(solution)/shard_map/all_to_all | solution.py:26
  171.1 12.9 %all-to-all-start.10 = ((f32[8,32,128]{2,1,0:T(8,128)}), f32[8,32,128]{2,1,0:T(8,128)S(1)}, u32[]{:S(2)}, u32[]{:S(2)}) async-start(f32[8,32,128]{2,1,0:T(8,128)} %broadcast_in_dim.24), calls=%async_computation.10 | async-start | bytes 262144 | tf_op jit(solution)/shard_map/all_to_all | solution.py:26
  197.2 11.6 %all-to-all-start.11 = ((f32[32,6,128]{2,1,0:T(8,128)}), f32[32,6,128]{2,1,0:T(8,128)S(1)}, u32[]{:S(2)}, u32[]{:S(2)}) async-start(f32[32,6,128]{2,1,0:T(8,128)} %reshape.123), calls=%async_computation.11 | async-start | bytes 262144 | tf_op jit(solution)/shard_map/all_to_all | solution.py:96
  208.8 14.5 %all-to-all-start.12 = ((f32[8,32,128]{2,1,0:T(8,128)}), f32[8,32,128]{2,1,0:T(8,128)S(1)}, u32[]{:S(2)}, u32[]{:S(2)}) async-start(f32[8,32,128]{2,1,0:T(8,128)} %bitcast.49), calls=%async_computation.12 | async-start | bytes 262144 | tf_op jit(solution)/shard_map/all_to_all | solution.py:20
  223.3 13.4 %all-to-all-start.14 = ((f32[32,6,128]{2,1,0:T(8,128)}), f32[32,6,128]{2,1,0:T(8,128)S(1)}, u32[]{:S(2)}, u32[]{:S(2)}) async-start(f32[32,6,128]{2,1,0:T(8,128)} %reshape.126), calls=%async_computation.14 | async-start | bytes 262144 | tf_op jit(solution)/shard_map/all_to_all | solution.py:125
  237.5 15.5 %all-to-all-start.13 = ((f32[32,32,128]{2,1,0:T(8,128)}), f32[32,32,128]{2,1,0:T(8,128)S(1)}, u32[]{:S(2)}, u32[]{:S(2)}) async-start(f32[32,32,128]{2,1,0:T(8,128)} %broadcast_in_dim.25), calls=%async_computation.13 | async-start | bytes 1048576 | tf_op jit(solution)/shard_map/all_to_all | solution.py:26
  254.4 13.0 %all-to-all-start.15 = ((f32[8,32,128]{2,1,0:T(8,128)}), f32[8,32,128]{2,1,0:T(8,128)S(1)}, u32[]{:S(2)}, u32[]{:S(2)}) async-start(f32[8,32,128]{2,1,0:T(8,128)} %broadcast_in_dim.26), calls=%async_computation.15 | async-start | bytes 262144 | tf_op jit(solution)/shard_map/all_to_all | solution.py:26
  (4 other events, 105.4 us)
where the time goes:
time: 273 us; the launch traced here: 271 us
  waiting for transfers between devices  93.7 us (34%)
  starting transfers between devices  85.1 us (31%)
  matrix products  62.1 us (23%)
  local copies, waits for them, and re-layouts  24 us (9%)
  other arithmetic  5.32 us (2%)
    all_to_all x6, waiting for transfers between devices, from_everyone(): return lax.all_to_all(copies, axis, split_axis=0, concat_axis=0, tiled=True)  32.7 us
    dot_general x3, matrix products, on_device(): jnp.einsum('bij,bj->bi', tail_blocks, tail_picked, precision=highest)  27.6 us
    all_to_all x3, waiting for transfers between devices, on_device(): lax.all_to_all(answers, 'rows', split_axis=0, concat_axis=0, tiled=True)  23.1 us
    all_to_all x6, starting transfers between devices, from_everyone(): return lax.all_to_all(copies, axis, split_axis=0, concat_axis=0, tiled=True)  22.7 us
    all_to_all x3, starting transfers between devices, sum_at_owner(): lax.all_to_all(pieces, axis, split_axis=0, concat_axis=0, tiled=True)  21.5 us
    all_to_all x3, waiting for transfers between devices, on_device(): lax.all_to_all(outgoing.reshape(row_devs, capacity, width), 'rows', split...  19.8 us
    all_to_all x3, waiting for transfers between devices, sum_at_owner(): lax.all_to_all(pieces, axis, split_axis=0, concat_axis=0, tiled=True)  18.1 us
    dot_general x3, matrix products, on_device(): jnp.einsum('bij,bi->bj', tail_blocks, duals[tail_row], precision=highest)  17.4 us
  transfers between devices with their start and end apart: 16, of which 12 were waited for; matrix products, arithmetic and copies ran while one was open for 19% of the time, Pallas kernels for 0%

commit v1 on v0

v1 whole, which is shorter than its diff:
```python
import jax
import jax.numpy as jnp
from jax import lax
from jax.experimental import pallas as pl
from jax.experimental.pallas import tpu as pltpu
from jax.sharding import PartitionSpec as P

ITERS = 3
PRIMAL = 0.25
DUAL = 0.25
MESH = pl.DeviceIdType.MESH
F32 = jnp.float32
BF16 = jnp.bfloat16

NT = 72
NH = 24
NR = 16
NC = 64
CAP = 6
BW = 128
ROWS = 32
HUBS = 8
TP = 80
HP = 32
PL = 8 * ROWS


def hops(d):
    return min(d, 4 - d)


OFFSETS = sorted(
    [(dy, dx, dc) for dy in range(4) for dx in range(4) for dc in range(2) if dy or dx or dc],
    key=lambda o: (-(hops(o[0]) + hops(o[1])), -o[2], o[0], o[1]),
)
HUB_OFFSETS = [4, 3, 5, 2, 6, 1, 7]


def iota(shape, dim):
    return lax.broadcasted_iota(jnp.int32, shape, dim)


def split3(a):
    hi = a.astype(BF16)
    rest = a - hi.astype(F32)
    mid = rest.astype(BF16)
    lo = (rest - mid.astype(F32)).astype(BF16)
    return hi, mid, lo


def mm(a, b):
    return jnp.dot(a, b, preferred_element_type=F32)


def kernel(
    tail_hbm, tail_row, owner_ref, tail_slot, hub_hbm, hub_row, hub_col,
    x_tail, cost_tail, upper_tail, x_hub, cost_hub, upper_hub, duals, demand,
    xt_out, xh_out, d_out,
    tb, hb, dbc,
    hub_out, hub_in, z_out, z_in, ag_out, ag_in,
    tail_out, tail_in, ans_out, ans_in,
    slot_out, slot_in, init_out, init_in, xf_out, xf_in,
    terms, hterms, picked, colbuf,
    s3, hp3, ct3, coll, st, rp, xh_state, d_state, dem_t,
    load_sem, s_sem, r_sem,
):
    me = lax.axis_index("rows")
    hub = lax.axis_index("hub")
    y, x, c = me // 8, lax.rem(me // 2, 4), lax.rem(me, 2)
    peers = [
        lax.rem(y + dy, 4) * 8 + lax.rem(x + dx, 4) * 2 + lax.rem(c + dc, 2) for dy, dx, dc in OFFSETS
    ]
    hub_peers = [lax.rem(hub + d, HUBS) for d in HUB_OFFSETS]

    def at8(i, n=8):
        return pl.ds(pl.multiple_of(i * 8, 8), n)

    loads = [pltpu.make_async_copy(hub_hbm, hb, load_sem.at[0])]
    loads[0].start()
    step = NT // 4
    for i in range(4):
        part = pl.ds(i * step, step)
        loads.append(pltpu.make_async_copy(tail_hbm.at[part], tb.at[part], load_sem.at[1 + i]))
        loads[-1].start()

    barrier = pltpu.get_barrier_semaphore()
    for p in peers:
        pl.semaphore_signal(barrier, inc=1, device_id={"rows": p}, device_id_type=MESH)
    for p in hub_peers:
        pl.semaphore_signal(barrier, inc=1, device_id={"hub": p}, device_id_type=MESH)

    def to_rows(src, dst, k):
        for p in peers:
            pltpu.make_async_remote_copy(
                src_ref=src(p), dst_ref=dst, send_sem=s_sem.at[k], recv_sem=r_sem.at[k],
                device_id={"rows": p}, device_id_type=MESH,
            ).start()

    def to_hubs(src, dst, k):
        for p in hub_peers:
            pltpu.make_async_remote_copy(
                src_ref=src, dst_ref=dst, send_sem=s_sem.at[k], recv_sem=r_sem.at[k],
                device_id={"hub": p}, device_id_type=MESH,
            ).start()

    def wait_bytes(ref, sem):
        pltpu.make_async_copy(ref, ref, sem).wait()

    for b in range(NT):
        colbuf[pl.ds(b, 1), :] = jnp.full((1, BW), tail_slot[b], jnp.int32).astype(F32)
    slot_col = jnp.where(iota((TP, BW), 0) < NT, colbuf[0:TP, :], 0.0)
    own = jnp.broadcast_to(owner_ref[...].astype(F32), (NT, BW))
    own_col = jnp.concatenate([own, jnp.full((BW - NT, BW), -1.0, F32)], axis=0)
    own_row = own_col.T
    sub, lane = iota((BW, BW), 0), iota((BW, BW), 1)
    before = jnp.where((own_col == own_row) & (lane < sub), 1.0, 0.0)
    within = jnp.sum(before, axis=1, keepdims=True)
    place = jnp.where(sub < NT, own_col * 8.0 + within, -1.0)
    place = place[0:TP, :]
    place3 = jnp.concatenate([place, place, place, jnp.full((16, BW), -1.0, F32)], axis=0)
    place_row = place3.T[0:1, :]
    s3[...] = jnp.where(iota((PL, 256), 0).astype(F32) == place_row, 1.0, 0.0).astype(BF16)
    st[...] = jnp.where(
        iota((TP, PL), 1).astype(F32) == jnp.concatenate([place, place], axis=1), 1.0, 0.0
    ).astype(BF16)
    zeros16 = jnp.zeros((16, BW), BF16)
    slot_b = slot_col.astype(BF16)
    zeros_tp = jnp.zeros((TP, BW), BF16)
    slot_out[...] = mm(s3[...], jnp.concatenate([slot_b, zeros_tp, zeros_tp, zeros16], axis=0))

    init_out[...] = jnp.zeros((8, BW), F32)
    init_out[0:1, :] = x_hub[pl.ds(me, 1), :]
    init_out[1:2, :] = cost_hub[pl.ds(me, 1), :]
    init_out[2:3, :] = upper_hub[pl.ds(me, 1), :]

    pl.semaphore_wait(barrier, len(OFFSETS) + len(HUB_OFFSETS))

    to_rows(lambda p: slot_out.at[at8(p, CAP), :], slot_in.at[at8(me, CAP), :], 15)
    to_hubs(init_out, init_in.at[at8(hub), :], 16)

    pos_row = jnp.full((1, BW), -1, jnp.int32)
    lane1 = iota((1, BW), 1)
    for k in range(NH):
        col = hub_col[k]
        pos = lax.rem(col, ROWS) * 8 + col // ROWS
        pos_row = jnp.where((lane1 % HP == k) & (lane1 < 3 * HP), pos, pos_row)
    hp3[...] = jnp.where(iota((PL, BW), 0) == pos_row, 1.0, 0.0).astype(BF16)

    for b in range(NT):
        colbuf[pl.ds(b, 1), :] = jnp.full((1, BW), tail_row[b], jnp.int32).astype(F32)
    for k in range(NH):
        colbuf[pl.ds(NT + k, 1), :] = jnp.full((1, BW), hub_row[k], jnp.int32).astype(F32)
    rp[...] = jnp.where(
        (colbuf[...] == lane.astype(F32)) & (sub < NT + NH), 1.0, 0.0
    ).astype(BF16)

    pad = jnp.zeros((BW - NR, BW), F32)
    dem_t[...] = jnp.concatenate([demand[...], pad], axis=0).T
    d_t = jnp.concatenate([duals[...], pad], axis=0).T
    d_state[...] = d_t
    for r in range(NR):
        dbc[r] = jnp.broadcast_to(d_t[:, r : r + 1], (BW, BW))

    terms[...] = jnp.zeros_like(terms)
    hterms[...] = jnp.zeros_like(hterms)
    xt_out[...] = x_tail[...]
    live = lax.rem(iota((PL, BW), 0), 8) < CAP

    loads[0].wait()

    def iteration(it, carry):
        def hub_adj(k, cc):
            hterms[pl.ds(k, 1), :] = jnp.sum(hb[k] * dbc[hub_row[k]], axis=0, keepdims=True)
            return cc

        lax.fori_loop(0, NH, hub_adj, 0, unroll=4)
        hi, mid, lo = split3(hterms[...])
        hub_out[it] = mm(hp3[...], jnp.concatenate([hi, mid, lo, jnp.zeros_like(hi)], axis=0))
        to_rows(lambda p: hub_out.at[it, at8(p), :], hub_in.at[it, at8(me), :], it)
        hub_in[it, at8(me), :] = hub_out[it, at8(me), :]

        @pl.when(it == 0)
        def _():
            for load in loads[1:]:
                load.wait()

        def tail_adj(b, cc):
            terms[pl.ds(b, 1), :] = jnp.sum(tb[b] * dbc[tail_row[b]], axis=0, keepdims=True)
            return cc

        lax.fori_loop(0, NT, tail_adj, 0, unroll=4)
        hi, mid, lo = split3(terms[...])
        tail_out[it] = mm(s3[...], jnp.concatenate([hi, mid, lo, zeros16], axis=0))
        to_rows(
            lambda p: tail_out.at[it, at8(p, CAP), :], tail_in.at[it, at8(me, CAP), :], 3 + it
        )
        tail_in[it, at8(me), :] = tail_out[it, at8(me), :]

        @pl.when(it == 0)
        def _():
            wait_bytes(slot_in.at[pl.ds(0, CAP * (ROWS - 1)), :], r_sem.at[15])
            slot_in[at8(me), :] = slot_out[at8(me), :]
            asked = jnp.where(live, slot_in[...], -1.0)
            asked_row = asked.T[0:NC, :]
            coll[...] = jnp.where(iota((NC, PL), 0).astype(F32) == asked_row, 1.0, 0.0).astype(BF16)
            lanes = iota((PL, 256), 1)
            asked2 = jnp.concatenate([asked, asked], axis=1)
            ct3[...] = jnp.where(
                (lax.rem(lanes, NC).astype(F32) == asked2) & (lanes < 3 * NC), 1.0, 0.0
            ).astype(BF16)
            wait_bytes(init_in.at[pl.ds(0, 8 * (HUBS - 1)), :], r_sem.at[16])
            init_in[at8(hub), :] = init_out[...]
            xh_state[...] = init_in[pl.ds(0, 8, stride=8), :]

        wait_bytes(hub_in.at[it, pl.ds(0, 8 * (ROWS - 1)), :], r_sem.at[it])
        part = jnp.sum(hub_in[it].reshape(ROWS, 8, BW), axis=0)
        z_out[it] = part
        to_hubs(z_out.at[it], z_in.at[it, at8(hub), :], 6 + it)
        z_in[it, at8(hub), :] = part

        wait_bytes(tail_in.at[it, pl.ds(0, CAP * (ROWS - 1)), :], r_sem.at[3 + it])
        hi, mid, lo = split3(jnp.where(live, tail_in[it], 0.0))
        cm = coll[...]
        image = mm(cm, hi) + mm(cm, mid) + mm(cm, lo)
        xt = xt_out[...]
        xn = jnp.minimum(jnp.maximum(xt - PRIMAL * (cost_tail[...] - image), 0.0), upper_tail[...])
        xt_out[...] = xn
        hi, mid, lo = split3(2.0 * xn - xt)
        ans_out[it] = mm(ct3[...], jnp.concatenate([hi, mid, lo, jnp.zeros_like(hi)], axis=0))
        to_rows(lambda p: ans_out.at[it, at8(p, CAP), :], ans_in.at[it, at8(me, CAP), :], 9 + it)
        ans_in[it, at8(me), :] = ans_out[it, at8(me), :]

        wait_bytes(z_in.at[it, pl.ds(0, 8 * (HUBS - 1)), :], r_sem.at[6 + it])
        total = jnp.sum(z_in[it].reshape(HUBS, 8, BW), axis=0)
        cost_h = init_in[pl.ds(1, 8, stride=8), :]
        upper_h = init_in[pl.ds(2, 8, stride=8), :]
        xh = xh_state[...]
        xhn = jnp.minimum(jnp.maximum(xh - PRIMAL * (cost_h - total), 0.0), upper_h)
        xh_state[...] = xhn
        extra = 2.0 * xhn - xh
        ag_out[it] = extra
        to_rows(lambda p: ag_out.at[it], ag_in.at[it, at8(me), :], 12 + it)
        ag_in[it, at8(me), :] = extra

        @pl.when(it == ITERS - 1)
        def _():
            xf_out[0] = xh_state[pl.ds(hub, 1), :]
            to_rows(lambda p: xf_out.at[0], xf_in.at[me], 17)
            xf_in[me] = xf_out[0]

        wait_bytes(ans_in.at[it, pl.ds(0, CAP * (ROWS - 1)), :], r_sem.at[9 + it])
        hi, mid, lo = split3(jnp.where(live, ans_in[it], 0.0))
        sm = st[...]
        picked[...] = mm(sm, hi) + mm(sm, mid) + mm(sm, lo)

        def tail_fwd(b, yy):
            prod = jnp.sum(tb[b] * picked[pl.ds(b, 1), :], axis=1, keepdims=True)
            return jnp.where(lane == b, prod, yy)

        yy = lax.fori_loop(0, NT, tail_fwd, jnp.zeros((BW, BW), F32), unroll=4)

        wait_bytes(ag_in.at[it, pl.ds(0, 8 * (ROWS - 1)), :], r_sem.at[12 + it])

        def hub_fwd(k, yy):
            col = hub_col[k]
            pos = lax.rem(col, ROWS) * 8 + col // ROWS
            prod = jnp.sum(hb[k] * ag_in[it, pl.ds(pos, 1), :], axis=1, keepdims=True)
            return jnp.where(lane == NT + k, prod, yy)

        yy = lax.fori_loop(0, NH, hub_fwd, yy, unroll=4)
        hi, mid, lo = split3(yy)
        rm = rp[...]
        primal = mm(hi, rm) + mm(mid, rm) + mm(lo, rm)
        d_new = jnp.maximum(d_state[...] + DUAL * (dem_t[...] - primal), 0.0)
        d_state[...] = d_new

        @pl.when(it < ITERS - 1)
        def _():
            for r in range(NR):
                dbc[r] = jnp.broadcast_to(d_new[:, r : r + 1], (BW, BW))

        return carry

    lax.fori_loop(0, ITERS, iteration, 0)

    d_out[...] = d_state[...].T[0:NR, :]
    wait_bytes(xf_in.at[pl.ds(0, ROWS - 1)], r_sem.at[17])
    for p in range(ROWS):
        xh_out[p : p + 1, :] = xf_in[p]

    full = hub_in.at[0, pl.ds(0, 8 * (ROWS - 1)), :]
    six = tail_in.at[0, pl.ds(0, CAP * (ROWS - 1)), :]
    seven = z_in.at[0, pl.ds(0, 8 * (HUBS - 1)), :]
    for it in range(ITERS):
        wait_bytes(full, s_sem.at[it])
        wait_bytes(six, s_sem.at[3 + it])
        wait_bytes(seven, s_sem.at[6 + it])
        wait_bytes(six, s_sem.at[9 + it])
        wait_bytes(full, s_sem.at[12 + it])
    wait_bytes(six, s_sem.at[15])
    wait_bytes(seven, s_sem.at[16])
    wait_bytes(xf_in.at[pl.ds(0, ROWS - 1)], s_sem.at[17])


def on_device(*args):
    vm = pl.BlockSpec(memory_space=pltpu.VMEM)
    sm = pl.BlockSpec(memory_space=pltpu.SMEM)
    hbm = pl.BlockSpec(memory_space=pltpu.HBM)
    v = lambda *s: pltpu.VMEM(s, F32)
    vb = lambda *s: pltpu.VMEM(s, BF16)
    return pl.pallas_call(
        kernel,
        out_shape=(
            jax.ShapeDtypeStruct((NC, BW), F32),
            jax.ShapeDtypeStruct((ROWS, BW), F32),
            jax.ShapeDtypeStruct((NR, BW), F32),
        ),
        in_specs=[hbm, sm, vm, sm, hbm, sm, sm] + [vm] * 8,
        out_specs=(vm, vm, vm),
        scratch_shapes=[
            v(NT, BW, BW), v(NH, BW, BW), v(NR, BW, BW),
            v(3, PL, BW), v(3, PL, BW), v(3, 8, BW), v(3, 64, BW), v(3, 8, BW), v(3, PL, BW),
            v(3, PL, BW), v(3, PL, BW), v(3, PL, BW), v(3, PL, BW),
            v(PL, BW), v(PL, BW), v(8, BW), v(64, BW), v(1, 1, BW), v(ROWS, 1, BW),
            v(TP, BW), v(HP, BW), v(TP, BW), v(BW, BW),
            vb(PL, 256), vb(PL, BW), vb(PL, 256), vb(NC, PL), vb(TP, PL), vb(BW, BW),
            v(8, BW), v(BW, BW), v(BW, BW),
            pltpu.SemaphoreType.DMA((5,)),
            pltpu.SemaphoreType.DMA((18,)),
            pltpu.SemaphoreType.DMA((18,)),
        ],
        compiler_params=pltpu.CompilerParams(
            collective_id=0, has_side_effects=True, vmem_limit_bytes=48 * 1024 * 1024
        ),
        name="pdhg",
    )(*args)


def solution(mesh):
    split = P(("rows", "hub"))
    split2 = P(("rows", "hub"), None)
    split3d = P(("rows", "hub"), None, None)
    hubs = P("hub", None)
    in_specs = (
        split3d, split, split2, split, split3d, split, split,
        split2, split2, split2, hubs, hubs, hubs, split2, split2,
    )
    return jax.shard_map(
        on_device, mesh=mesh, in_specs=in_specs, out_specs=(split2, hubs, split2), check_vma=False
    )
```

time: 273 us -> 74.8 us (0.27)
  waiting for transfers between devices: 93.7 us -> 0 us
  starting transfers between devices: 85.1 us -> 0 us
  matrix products: 62.1 us -> 0 us
  Pallas kernels: 0 us -> 61.2 us
  local copies, waits for them, and re-layouts: 24 us -> 12.4 us
  other arithmetic: 5.32 us -> 0 us
    all_to_all x16 -> x0, waiting for transfers between devices: 93.7 us -> none  [the longest x6 32.7 us: from_everyone(): return lax.all_to_all(copies, axis, split_axis=0, concat_axis=0, tiled=True)]
    all_to_all x16 -> x0, starting transfers between devices: 85.1 us -> none  [the longest x6 22.7 us: from_everyone(): return lax.all_to_all(copies, axis, split_axis=0, concat_axis=0, tiled=True)]
    dot_general x24 -> x0, matrix products: 62.1 us -> none  [the longest x3 27.6 us: on_device(): jnp.einsum('bij,bj->bi', tail_blocks, tail_picked, precision=highest)]
    pallas_call x0 -> x1, Pallas kernels: none -> 61.2 us  [on_device(): pl.pallas_call(kernel, out_shape=(jax.ShapeDtypeStruct((NC, BW), F32), ja...]
    unnamed x24 -> x30, local copies, waits for them, and re-layouts: 0.07 us -> 12.4 us
    gather x15 -> x0, local copies, waits for them, and re-layouts: 10.6 us -> none  [the longest x3 2.51 us: on_device(): duals[tail_row]]
    broadcast_in_dim x6 -> x0, local copies, waits for them, and re-layouts: 4.55 us -> none  [from_everyone(): copies = jnp.broadcast_to(shard, (lax.axis_size(axis), *shard.shape))]
    reshape x13 -> x0, local copies, waits for them, and re-layouts: 4.16 us -> none  [the longest x3 1.99 us: on_device(): outgoing.reshape(row_devs, capacity, width)]
  transfers between devices with their start and end apart: 16 -> 0, of which waited for: 12 -> 0; matrix products, arithmetic and copies ran while one was open for 19% -> 0% of each run, Pallas kernels for 0% -> 0%
where the time goes in v1:
time: 74.8 us; the launch traced here: 74.2 us
  Pallas kernels  61.2 us (82%)
  local copies, waits for them, and re-layouts  12.4 us (17%)
    pallas_call x1, Pallas kernels, on_device(): pl.pallas_call(kernel, out_shape=(jax.ShapeDtypeStruct((NC, BW), F32), ja...  61.2 us
    unnamed x30, local copies, waits for them, and re-layouts  12.4 us

profile of v1, /device:TPU:1, one launch (start us, length us, event | category | flops | bytes accessed | tf_op | source)
XLA Modules:
  0.0 74.2 jit_solution(25179013056683139)
XLA Ops:
  0.6 0.7 %copy.18.owner_ref = s32[72,1]{1,0:T(8,128)S(1)} copy(s32[72,1]{0,1:T(1,128)} %param.17) | data formatting | bytes 576 | tf_op args[2]
  1.4 0.0 copy-start
  1.4 1.4 %copy-done = f32[24,128,128]{2,1,0:T(8,128)S(1)} copy-done((f32[24,128,128]{2,1,0:T(8,128)S(1)}, f32[24,128,128]{2,1,0:T(8,128)}, u32[]{:S(2)}) %copy-start) | copy-done | bytes 1572888
  2.8 0.0 copy-start.1
  2.8 0.8 %copy-done.1 = f32[64,128]{1,0:T(8,128)S(1)} copy-done((f32[64,128]{1,0:T(8,128)S(1)}, f32[64,128]{1,0:T(8,128)}, u32[]{:S(2)}) %copy-start.1) | copy-done | bytes 32792
  3.5 0.0 copy-start.2
  3.5 0.8 %copy-done.2 = f32[64,128]{1,0:T(8,128)S(1)} copy-done((f32[64,128]{1,0:T(8,128)S(1)}, f32[64,128]{1,0:T(8,128)}, u32[]{:S(2)}) %copy-start.2) | copy-done | bytes 32792
  4.3 0.0 copy-start.3
  4.3 0.8 %copy-done.3 = f32[64,128]{1,0:T(8,128)S(1)} copy-done((f32[64,128]{1,0:T(8,128)S(1)}, f32[64,128]{1,0:T(8,128)}, u32[]{:S(2)}) %copy-start.3) | copy-done | bytes 32792
  5.1 0.0 copy-start.4
  5.1 0.7 copy-done.4
  5.8 0.0 copy-start.5
  5.8 0.7 copy-done.5
  6.5 0.7 copy-done.6
  7.2 0.7 copy-done.7
  7.9 0.7 copy-done.8
  8.6 0.7 copy-done.9
  9.3 0.7 copy-done.10
  9.9 0.7 copy-done.11
  10.6 0.7 copy-done.12
  11.2 61.2 %pdhg.1 = (f32[64,128]{1,0:T(8,128)S(1)}, f32[32,128]{1,0:T(8,128)S(1)}, f32[16,128]{1,0:T(8,128)S(1)}) custom-call(f32[72,128,128]{2,1,0:T(8,128)} %tail_hbm.1, s32[72]{0:T(128)S(1)} %copy-done.9, s32[72,1]{1,0:T(8,128)S(1)} %copy.18.owner_ref, s32[72]{0:T(128)S(1)} %copy-done.10, f32[24,128,128]{2,1,0:T(8,128)S(1)} %copy-done, s32[24]{0:T(128)S(1)} %copy-done.11, ...), custom_call_target="tpu_custom_call" | custom-call | tf_op jit(solution)/shard_map/pdhg/pallas_call | solution.py:311
  72.4 0.6 copy.22
  73.0 0.6 copy.23
  73.6 0.6 copy.24
  (7 shorter events, 0.0 us)
Async XLA Ops:
  1.4 1.4 %copy-start = (f32[24,128,128]{2,1,0:T(8,128)S(1)}, f32[24,128,128]{2,1,0:T(8,128)}, u32[]{:S(2)}) copy-start(f32[24,128,128]{2,1,0:T(8,128)} %hub_hbm.1) | copy-start | bytes 4718596
  2.8 0.8 %copy-start.1 = (f32[64,128]{1,0:T(8,128)S(1)}, f32[64,128]{1,0:T(8,128)}, u32[]{:S(2)}) copy-start(f32[64,128]{1,0:T(8,128)} %x_tail.1) | copy-start | bytes 98308
  3.5 0.8 %copy-start.2 = (f32[64,128]{1,0:T(8,128)S(1)}, f32[64,128]{1,0:T(8,128)}, u32[]{:S(2)}) copy-start(f32[64,128]{1,0:T(8,128)} %cost_tail.1) | copy-start | bytes 98308
  4.3 0.8 %copy-start.3 = (f32[64,128]{1,0:T(8,128)S(1)}, f32[64,128]{1,0:T(8,128)}, u32[]{:S(2)}) copy-start(f32[64,128]{1,0:T(8,128)} %upper_tail.1) | copy-start | bytes 98308
  5.1 0.7 copy-start.4
  5.8 0.7 copy-start.5
  6.5 0.7 copy-start.6
  7.2 0.7 copy-start.7
  7.9 0.7 copy-start.8
  8.6 0.7 copy-start.9
  9.3 0.7 copy-start.10
  9.9 0.7 copy-start.11
  10.6 0.7 copy-start.12

commit v2 on v1

--- a/solution.py
+++ b/solution.py
@@ -20,6 +20,7 @@
 BW = 128
 ROWS = 32
 HUBS = 8
+CHUNKS = 12
 TP = 80
 HP = 32
 PL = 8 * ROWS
@@ -52,16 +53,34 @@
     return jnp.dot(a, b, preferred_element_type=F32)
 
 
+class Scope:
+    def __init__(self):
+        self.now = None
+
+    def leave(self):
+        if self.now is not None:
+            self.now.__exit__(None, None, None)
+        self.now = None
+
+    def enter(self, name):
+        self.leave()
+        self.now = jax.named_scope(name)
+        self.now.__enter__()
+
+
 def kernel(
-    tail_hbm, tail_row, owner_ref, tail_slot, hub_hbm, hub_row, hub_col,
-    x_tail, cost_tail, upper_tail, x_hub, cost_hub, upper_hub, duals, demand,
+    tail_hbm, tail_row_hbm, owner_hbm, tail_slot_hbm, hub_hbm, hub_row_hbm, hub_col_hbm,
+    x_tail_hbm, cost_tail_hbm, upper_tail_hbm, x_hub_hbm, cost_hub_hbm, upper_hub_hbm,
+    duals_hbm, demand_hbm,
     xt_out, xh_out, d_out,
+    tail_row, owner, tail_slot, hub_row, hub_col,
+    cost_tail, upper_tail, x_hub, cost_hub, upper_hub, duals, demand,
     tb, hb, dbc,
     hub_out, hub_in, z_out, z_in, ag_out, ag_in,
     tail_out, tail_in, ans_out, ans_in,
     slot_out, slot_in, init_out, init_in, xf_out, xf_in,
-    terms, hterms, picked, colbuf,
-    s3, hp3, ct3, coll, st, rp, xh_state, d_state, dem_t,
+    terms, hterms, picked, colbuf, idx_v, idx, tacc, hacc, dem,
+    s3, hp3, ct3, coll, st, xh_state,
     load_sem, s_sem, r_sem,
 ):
     me = lax.axis_index("rows")
@@ -75,13 +94,22 @@
     def at8(i, n=8):
         return pl.ds(pl.multiple_of(i * 8, 8), n)
 
-    loads = [pltpu.make_async_copy(hub_hbm, hb, load_sem.at[0])]
-    loads[0].start()
-    step = NT // 4
-    for i in range(4):
-        part = pl.ds(i * step, step)
-        loads.append(pltpu.make_async_copy(tail_hbm.at[part], tb.at[part], load_sem.at[1 + i]))
-        loads[-1].start()
+    pairs = [
+        (owner_hbm, owner), (tail_slot_hbm, tail_slot), (hub_col_hbm, hub_col),
+        (tail_row_hbm, tail_row), (hub_row_hbm, hub_row),
+        (x_hub_hbm, x_hub), (cost_hub_hbm, cost_hub), (upper_hub_hbm, upper_hub),
+        (duals_hbm, duals), (demand_hbm, demand), (hub_hbm, hb),
+        (x_tail_hbm, xt_out), (cost_tail_hbm, cost_tail), (upper_tail_hbm, upper_tail),
+    ]
+    step = NT // CHUNKS
+    pairs += [
+        (tail_hbm.at[pl.ds(i * step, step)], tb.at[pl.ds(i * step, step)]) for i in range(CHUNKS)
+    ]
+    scope = Scope()
+    scope.enter("start")
+    loads = [pltpu.make_async_copy(s, d, load_sem.at[i]) for i, (s, d) in enumerate(pairs)]
+    for load in loads:
+        load.start()
 
     barrier = pltpu.get_barrier_semaphore()
     for p in peers:
@@ -106,11 +134,14 @@
     def wait_bytes(ref, sem):
         pltpu.make_async_copy(ref, ref, sem).wait()
 
+    loads[0].wait()
+    loads[1].wait()
     for b in range(NT):
         colbuf[pl.ds(b, 1), :] = jnp.full((1, BW), tail_slot[b], jnp.int32).astype(F32)
     slot_col = jnp.where(iota((TP, BW), 0) < NT, colbuf[0:TP, :], 0.0)
-    own = jnp.broadcast_to(owner_ref[...].astype(F32), (NT, BW))
-    own_col = jnp.concatenate([own, jnp.full((BW - NT, BW), -1.0, F32)], axis=0)
+    for b in range(NT):
+        colbuf[pl.ds(b, 1), :] = jnp.full((1, BW), owner[b], jnp.int32).astype(F32)
+    own_col = jnp.where(iota((BW, BW), 0) < NT, colbuf[...], -1.0)
     own_row = own_col.T
     sub, lane = iota((BW, BW), 0), iota((BW, BW), 1)
     before = jnp.where((own_col == own_row) & (lane < sub), 1.0, 0.0)
@@ -128,16 +159,15 @@
     zeros_tp = jnp.zeros((TP, BW), BF16)
     slot_out[...] = mm(s3[...], jnp.concatenate([slot_b, zeros_tp, zeros_tp, zeros16], axis=0))
 
+    for load in loads[5:8]:
+        load.wait()
     init_out[...] = jnp.zeros((8, BW), F32)
     init_out[0:1, :] = x_hub[pl.ds(me, 1), :]
     init_out[1:2, :] = cost_hub[pl.ds(me, 1), :]
     init_out[2:3, :] = upper_hub[pl.ds(me, 1), :]
 
-    pl.semaphore_wait(barrier, len(OFFSETS) + len(HUB_OFFSETS))
-
-    to_rows(lambda p: slot_out.at[at8(p, CAP), :], slot_in.at[at8(me, CAP), :], 15)
-    to_hubs(init_out, init_in.at[at8(hub), :], 16)
-
+    for load in loads[2:5]:
+        load.wait()
     pos_row = jnp.full((1, BW), -1, jnp.int32)
     lane1 = iota((1, BW), 1)
     for k in range(NH):
@@ -146,42 +176,96 @@
         pos_row = jnp.where((lane1 % HP == k) & (lane1 < 3 * HP), pos, pos_row)
     hp3[...] = jnp.where(iota((PL, BW), 0) == pos_row, 1.0, 0.0).astype(BF16)
 
+    subf, lanef = sub.astype(F32), lane.astype(F32)
+
+    def by_row(count, at, values):
+        held = jnp.where(sub < count, colbuf[...], 1000.0)
+        other = held.T
+        rank = jnp.sum(
+            jnp.where((other < held) | ((other == held) & (lane < sub)), 1.0, 0.0),
+            axis=1, keepdims=True,
+        )
+        here = rank == lanef
+
+        def listed(v):
+            return jnp.sum(jnp.where(here, v, 0.0), axis=0, keepdims=True)
+
+        rows = listed(held)
+        last = jnp.sum(jnp.where(held <= lanef, 1.0, 0.0), axis=0, keepdims=True)
+        some = jnp.sum(jnp.where(held == lanef, 1.0, 0.0), axis=0, keepdims=True)
+        keep = (rows == pltpu.roll(rows, 1, 1)) & (lane1 > 0)
+        lists = [
+            listed(subf),
+            jnp.where(keep, 1.0, 0.0),
+            jnp.where(some > 0.0, last - 1.0, 1.0 * count),
+        ] + [listed(v) for v in values]
+        for i, v in enumerate(lists):
+            idx_v[at + i : at + i + 1, :] = v.astype(jnp.int32)
+
     for b in range(NT):
         colbuf[pl.ds(b, 1), :] = jnp.full((1, BW), tail_row[b], jnp.int32).astype(F32)
+    by_row(NT, 0, [])
     for k in range(NH):
-        colbuf[pl.ds(NT + k, 1), :] = jnp.full((1, BW), hub_row[k], jnp.int32).astype(F32)
-    rp[...] = jnp.where(
-        (colbuf[...] == lane.astype(F32)) & (sub < NT + NH), 1.0, 0.0
-    ).astype(BF16)
-
+        col = hub_col[k]
+        pos = lax.rem(col, ROWS) * 8 + col // ROWS
+        colbuf[pl.ds(k, 1), :] = jnp.full((1, BW), pos, jnp.int32).astype(F32)
+    pos_col = jnp.where(sub < NH, colbuf[...], 0.0)
+    for k in range(NH):
+        colbuf[pl.ds(k, 1), :] = jnp.full((1, BW), hub_row[k], jnp.int32).astype(F32)
+    by_row(NH, 3, [pos_col])
+    idx_v[7:8, :] = jnp.zeros((1, BW), jnp.int32)
+    to_scalars = pltpu.make_async_copy(idx_v, idx, load_sem.at[14 + CHUNKS])
+    to_scalars.start()
+    tacc[NT] = jnp.zeros((BW, BW), F32)
+    hacc[NH] = jnp.zeros((BW, BW), F32)
+
+    loads[8].wait()
+    loads[9].wait()
     pad = jnp.zeros((BW - NR, BW), F32)
-    dem_t[...] = jnp.concatenate([demand[...], pad], axis=0).T
     d_t = jnp.concatenate([duals[...], pad], axis=0).T
-    d_state[...] = d_t
+    dem_t = jnp.concatenate([demand[...], pad], axis=0).T
     for r in range(NR):
         dbc[r] = jnp.broadcast_to(d_t[:, r : r + 1], (BW, BW))
+    for r in range(NR):
+        dem[r] = jnp.broadcast_to(dem_t[:, r : r + 1], (BW, BW))
 
     terms[...] = jnp.zeros_like(terms)
     hterms[...] = jnp.zeros_like(hterms)
-    xt_out[...] = x_tail[...]
     live = lax.rem(iota((PL, BW), 0), 8) < CAP
 
-    loads[0].wait()
-
-    def iteration(it, carry):
-        def hub_adj(k, cc):
-            hterms[pl.ds(k, 1), :] = jnp.sum(hb[k] * dbc[hub_row[k]], axis=0, keepdims=True)
-            return cc
-
-        lax.fori_loop(0, NH, hub_adj, 0, unroll=4)
+    def listed_at(i, k, top):
+        return jnp.minimum(jnp.maximum(idx[i, k], 0), top)
+
+    def hub_adjoint(it):
+        for k in range(NH):
+            hterms[k : k + 1, :] = jnp.sum(hb[k] * dbc[hub_row[k]], axis=0, keepdims=True)
         hi, mid, lo = split3(hterms[...])
         hub_out[it] = mm(hp3[...], jnp.concatenate([hi, mid, lo, jnp.zeros_like(hi)], axis=0))
+
+    scope.enter("wait_hb")
+    loads[10].wait()
+    scope.enter("adj_hub0")
+    hub_adjoint(0)
+    to_scalars.wait()
+
+    scope.enter("wait_barrier")
+    pl.semaphore_wait(barrier, len(OFFSETS) + len(HUB_OFFSETS))
+    scope.leave()
+
+    def iteration(it, carry):
+        scope.enter("rs_send")
         to_rows(lambda p: hub_out.at[it, at8(p), :], hub_in.at[it, at8(me), :], it)
         hub_in[it, at8(me), :] = hub_out[it, at8(me), :]
 
         @pl.when(it == 0)
         def _():
-            for load in loads[1:]:
+            to_hubs(init_out, init_in.at[at8(hub), :], 16)
+            to_rows(lambda p: slot_out.at[at8(p, CAP), :], slot_in.at[at8(me, CAP), :], 15)
+
+        scope.enter("adj_tail")
+        @pl.when(it == 0)
+        def _():
+            for load in loads[11:]:
                 load.wait()
 
         def tail_adj(b, cc):
@@ -212,13 +296,17 @@
             init_in[at8(hub), :] = init_out[...]
             xh_state[...] = init_in[pl.ds(0, 8, stride=8), :]
 
+        scope.enter("wait_rs")
         wait_bytes(hub_in.at[it, pl.ds(0, 8 * (ROWS - 1)), :], r_sem.at[it])
+        scope.enter("z_send")
         part = jnp.sum(hub_in[it].reshape(ROWS, 8, BW), axis=0)
         z_out[it] = part
         to_hubs(z_out.at[it], z_in.at[it, at8(hub), :], 6 + it)
         z_in[it, at8(hub), :] = part
 
+        scope.enter("wait_tail")
         wait_bytes(tail_in.at[it, pl.ds(0, CAP * (ROWS - 1)), :], r_sem.at[3 + it])
+        scope.enter("tail_update")
         hi, mid, lo = split3(jnp.where(live, tail_in[it], 0.0))
         cm = coll[...]
         image = mm(cm, hi) + mm(cm, mid) + mm(cm, lo)
@@ -230,7 +318,9 @@
         to_rows(lambda p: ans_out.at[it, at8(p, CAP), :], ans_in.at[it, at8(me, CAP), :], 9 + it)
         ans_in[it, at8(me), :] = ans_out[it, at8(me), :]
 
+        scope.enter("wait_z")
         wait_bytes(z_in.at[it, pl.ds(0, 8 * (HUBS - 1)), :], r_sem.at[6 + it])
+        scope.enter("hub_update")
         total = jnp.sum(z_in[it].reshape(HUBS, 8, BW), axis=0)
         cost_h = init_in[pl.ds(1, 8, stride=8), :]
         upper_h = init_in[pl.ds(2, 8, stride=8), :]
@@ -248,42 +338,51 @@
             to_rows(lambda p: xf_out.at[0], xf_in.at[me], 17)
             xf_in[me] = xf_out[0]
 
+        scope.enter("wait_ans")
         wait_bytes(ans_in.at[it, pl.ds(0, CAP * (ROWS - 1)), :], r_sem.at[9 + it])
+        scope.enter("fwd_tail")
         hi, mid, lo = split3(jnp.where(live, ans_in[it], 0.0))
         sm = st[...]
         picked[...] = mm(sm, hi) + mm(sm, mid) + mm(sm, lo)
 
-        def tail_fwd(b, yy):
-            prod = jnp.sum(tb[b] * picked[pl.ds(b, 1), :], axis=1, keepdims=True)
-            return jnp.where(lane == b, prod, yy)
-
-        yy = lax.fori_loop(0, NT, tail_fwd, jnp.zeros((BW, BW), F32), unroll=4)
-
+        def tail_fwd(k, acc):
+            i = listed_at(0, k, NT - 1)
+            acc = acc * idx[1, k].astype(F32) + tb[i] * picked[pl.ds(i, 1), :]
+            tacc[k] = acc
+            return acc
+
+        lax.fori_loop(0, NT, tail_fwd, jnp.zeros((BW, BW), F32), unroll=8)
+
+        scope.enter("wait_ag")
         wait_bytes(ag_in.at[it, pl.ds(0, 8 * (ROWS - 1)), :], r_sem.at[12 + it])
 
-        def hub_fwd(k, yy):
-            col = hub_col[k]
-            pos = lax.rem(col, ROWS) * 8 + col // ROWS
-            prod = jnp.sum(hb[k] * ag_in[it, pl.ds(pos, 1), :], axis=1, keepdims=True)
-            return jnp.where(lane == NT + k, prod, yy)
-
-        yy = lax.fori_loop(0, NH, hub_fwd, yy, unroll=4)
-        hi, mid, lo = split3(yy)
-        rm = rp[...]
-        primal = mm(hi, rm) + mm(mid, rm) + mm(lo, rm)
-        d_new = jnp.maximum(d_state[...] + DUAL * (dem_t[...] - primal), 0.0)
-        d_state[...] = d_new
+        scope.enter("fwd_hub")
+        acc = jnp.zeros((BW, BW), F32)
+        for k in range(NH):
+            acc = acc * idx[4, k].astype(F32) + hb[listed_at(3, k, NH - 1)] * ag_in[it, pl.ds(listed_at(6, k, PL - 1), 1), :]
+            hacc[k] = acc
+        scope.enter("dual")
+        for r in range(NR):
+            image = jnp.sum(
+                tacc[listed_at(2, r, NT)] + hacc[listed_at(5, r, NH)], axis=1, keepdims=True
+            )
+            dbc[r] = jnp.maximum(dbc[r] + DUAL * (dem[r] - image), 0.0)
 
         @pl.when(it < ITERS - 1)
         def _():
-            for r in range(NR):
-                dbc[r] = jnp.broadcast_to(d_new[:, r : r + 1], (BW, BW))
-
+            with jax.named_scope("adj_hub"):
+                hub_adjoint(it + 1)
+
+        scope.leave()
         return carry
 
     lax.fori_loop(0, ITERS, iteration, 0)
 
-    d_out[...] = d_state[...].T[0:NR, :]
+    scope.enter("finish")
+    narrow = jnp.zeros((BW, BW), F32)
+    for r in range(NR):
+        narrow = jnp.where(lane == r, dbc[r], narrow)
+    d_out[...] = narrow.T[0:NR, :]
     wait_bytes(xf_in.at[pl.ds(0, ROWS - 1)], r_sem.at[17])
     for p in range(ROWS):
         xh_out[p : p + 1, :] = xf_in[p]
@@ -300,40 +399,64 @@
     wait_bytes(six, s_sem.at[15])
     wait_bytes(seven, s_sem.at[16])
     wait_bytes(xf_in.at[pl.ds(0, ROWS - 1)], s_sem.at[17])
+    scope.leave()
+
+
+def writer(a_ref, b_ref, c_ref, a_out, b_out, c_out, sem):
+    copies = [
+        pltpu.make_async_copy(src, dst, sem.at[i])
+        for i, (src, dst) in enumerate([(a_ref, a_out), (b_ref, b_out), (c_ref, c_out)])
+    ]
+    for copy in copies:
+        copy.start()
+    for copy in copies:
+        copy.wait()
 
 
 def on_device(*args):
+    args = list(args)
+    args[2] = args[2].reshape(NT)
     vm = pl.BlockSpec(memory_space=pltpu.VMEM)
-    sm = pl.BlockSpec(memory_space=pltpu.SMEM)
     hbm = pl.BlockSpec(memory_space=pltpu.HBM)
+    args = [pltpu.with_memory_space_constraint(a, pltpu.HBM) for a in args]
     v = lambda *s: pltpu.VMEM(s, F32)
+    si = lambda n: pltpu.SMEM((n,), jnp.int32)
     vb = lambda *s: pltpu.VMEM(s, BF16)
-    return pl.pallas_call(
+    outs = [(NC, BW), (ROWS, BW), (NR, BW)]
+    held = pl.pallas_call(
         kernel,
-        out_shape=(
-            jax.ShapeDtypeStruct((NC, BW), F32),
-            jax.ShapeDtypeStruct((ROWS, BW), F32),
-            jax.ShapeDtypeStruct((NR, BW), F32),
-        ),
-        in_specs=[hbm, sm, vm, sm, hbm, sm, sm] + [vm] * 8,
+        out_shape=tuple(pltpu.VMEM(s, F32) for s in outs),
+        in_specs=[hbm] * 15,
         out_specs=(vm, vm, vm),
         scratch_shapes=[
+            si(NT), si(NT), si(NT), si(NH), si(NH),
+            v(NC, BW), v(NC, BW), v(ROWS, BW), v(ROWS, BW), v(ROWS, BW), v(NR, BW), v(NR, BW),
             v(NT, BW, BW), v(NH, BW, BW), v(NR, BW, BW),
             v(3, PL, BW), v(3, PL, BW), v(3, 8, BW), v(3, 64, BW), v(3, 8, BW), v(3, PL, BW),
             v(3, PL, BW), v(3, PL, BW), v(3, PL, BW), v(3, PL, BW),
             v(PL, BW), v(PL, BW), v(8, BW), v(64, BW), v(1, 1, BW), v(ROWS, 1, BW),
             v(TP, BW), v(HP, BW), v(TP, BW), v(BW, BW),
-            vb(PL, 256), vb(PL, BW), vb(PL, 256), vb(NC, PL), vb(TP, PL), vb(BW, BW),
-            v(8, BW), v(BW, BW), v(BW, BW),
-            pltpu.SemaphoreType.DMA((5,)),
+            pltpu.VMEM((8, BW), jnp.int32), pltpu.SMEM((8, BW), jnp.int32),
+            v(NT + 1, BW, BW), v(NH + 1, BW, BW), v(NR, BW, BW),
+            vb(PL, 256), vb(PL, BW), vb(PL, 256), vb(NC, PL), vb(TP, PL), v(8, BW),
+            pltpu.SemaphoreType.DMA((15 + CHUNKS,)),
             pltpu.SemaphoreType.DMA((18,)),
             pltpu.SemaphoreType.DMA((18,)),
         ],
         compiler_params=pltpu.CompilerParams(
-            collective_id=0, has_side_effects=True, vmem_limit_bytes=48 * 1024 * 1024
+            collective_id=0, has_side_effects=True, vmem_limit_bytes=32 * 1024 * 1024
         ),
         name="pdhg",
     )(*args)
+    return pl.pallas_call(
+        writer,
+        out_shape=tuple(jax.ShapeDtypeStruct(s, F32) for s in outs),
+        in_specs=[vm, vm, vm],
+        out_specs=(hbm, hbm, hbm),
+        scratch_shapes=[pltpu.SemaphoreType.DMA((3,))],
+        compiler_params=pltpu.CompilerParams(vmem_limit_bytes=1024 * 1024),
+        name="writer",
+    )(*held)
 
 
 def solution(mesh):

time: 74.8 us -> 60 us (0.80)
  local copies, waits for them, and re-layouts: 12.4 us -> 0 us
  Pallas kernels: 61.2 us -> 59.3 us
    unnamed x30 -> x0, local copies, waits for them, and re-layouts: 12.4 us -> none
    pallas_call x1 -> x2, Pallas kernels: 61.2 us -> 59.3 us  [the longest x1 58.6 us: on_device(): pl.pallas_call(kernel, out_shape=tuple((pltpu.VMEM(s, F32) for s in outs)...]
where the time goes in v2:
time: 60 us; the launch traced here: 59.9 us
  Pallas kernels  59.3 us (99%)
  between operations  0.64 us (1%)
    pallas_call x1, Pallas kernels, on_device(): pl.pallas_call(kernel, out_shape=tuple((pltpu.VMEM(s, F32) for s in outs)...  58.6 us

profile of v2, /device:TPU:1, one launch (start us, length us, event | category | flops | bytes accessed | tf_op | source)
XLA Modules:
  0.0 59.9 jit_solution(13236451746370980183)
XLA Ops:
  0.6 58.6 %pdhg.1 = (f32[64,128]{1,0:T(8,128)S(1)}, f32[32,128]{1,0:T(8,128)S(1)}, f32[16,128]{1,0:T(8,128)S(1)}) custom-call(f32[72,128,128]{2,1,0:T(8,128)} %tail_hbm.1, s32[72]{0:T(128)} %tail_row_hbm.1, s32[72]{0:T(128)} %bitcast.1, s32[72]{0:T(128)} %tail_slot_hbm.1, f32[24,128,128]{2,1,0:T(8,128)} %hub_hbm.1, s32[24]{0:T(128)} %hub_row_hbm.1, s32[24]{0:T(128)} %hub_col_hbm.1, ...), custom_call_target="tpu_custom_call" | custom-call | tf_op jit(solution)/shard_map/pdhg/pallas_call | solution.py:426
  59.3 0.6 %writer.1 = (f32[64,128]{1,0:T(8,128)}, f32[32,128]{1,0:T(8,128)}, f32[16,128]{1,0:T(8,128)}) custom-call(f32[64,128]{1,0:T(8,128)S(1)} %get-tuple-element.6.a_ref, f32[32,128]{1,0:T(8,128)S(1)} %get-tuple-element.7.b_ref, f32[16,128]{1,0:T(8,128)S(1)} %get-tuple-element.8.c_ref), custom_call_target="tpu_custom_call" | custom-call | tf_op jit(solution)/shard_map/writer/pallas_call | solution.py:451
